TPU v7x, 32 devices: a whole 2x2x4 slice. The times are simulated.
32 devices in a mesh: row: 8 (over y, x, core), col: 4 (over z).
Axes of the slice: x: 2, y: 2, z: 4, core: 2. Of those that a mesh axis runs over, the one named last changes fastest.
Arguments:
- source_points: float32 [3, 32768], P(None, 'col'), may hold values from 0 to 1
- source_areas: float32 [32768], P('col'), may hold values from 0.02 to 0.2
- source_fill: int32 [128], P('col'), may hold values from 128 to 256
- target_points: float32 [3, 32768], P(None, 'row'), may hold values from 0 to 1
- target_fill: int32 [128], P('row'), may hold values from 128 to 256
- charges: bfloat16 [64, 32768], P('row', 'col'), may hold values from -6 to 6
- near_fill: int32 [8, 4], P('row', 'col'), may hold values from 32 to 256, as said below
- near_source: int32 [8, 1024], P('row', 'col'), may hold values from 0 to 31
- near_target: int32 [8, 1024], P('row', 'col'), may hold values from 0 to 15
- far_source: int32 [8, 384], P('row', 'col'), may hold values from 0 to 31
- far_target: int32 [8, 384], P('row', 'col'), may hold values from 0 to 15
- far_rank: int32 [8, 384], P('row', 'col'), may hold values from 8 to 32
- left_basis: bfloat16 [8, 384, 32, 256], P('row', 'col'), may hold values from -0.25 to 0.25
- right_basis: bfloat16 [8, 384, 32, 256], P('row', 'col'), may hold values from -0.375 to 0.375
Outputs:
- potential: float32 [64, 32768], P('col', 'row')
Inputs may be any that keep to these rules, and one draw needn't show every extreme that they name: `near_fill`: used slots are the first ones of a device; in every row some device uses all 256. `near_source`: index among the 32 source leaves of the device's column group. `near_target`: index among the 16 target leaves of the device's row group. `far_source`: index among the 32 source leaves of the device's column group. `far_target`: index among the 16 target leaves of the device's row group. `far_rank`: factor rows from the rank on are padding.
All inputs are finite; a program needn't handle non-finite values.
Results may differ from a plain program's by a relative error of at most 0.0029.
Values may be sent and summed in bfloat16 or wider, within the bound.
No kernel may reach another device: no remote copies, remote signals or barrier semaphores. Data moves between devices by JAX's collectives and lax.ppermute only.
A program may use at most 64 MiB of HBM per device.

v0:
```python
import functools

import jax
import jax.numpy as jnp
from jax import lax
from jax.experimental import pallas as pl
from jax.experimental.pallas import tpu as pltpu
from jax.sharding import PartitionSpec as P

INV_FOUR_PI = 0.07957747154594767
SOFTENING_SQ = 0.0025
F32 = jnp.float32
BF16 = jnp.bfloat16
VMEM_LIMIT = 60 << 20


def split3(value):
    first = value.astype(BF16).astype(F32)
    rest = value - first
    second = rest.astype(BF16).astype(F32)
    return first, second, rest - second


def feature_rows(rows):
    count = rows[0].shape[1]
    index = lax.broadcasted_iota(jnp.int32, (8, count), 0)
    out = jnp.zeros((8, count), F32)
    for position, row in enumerate(rows):
        out = jnp.where(index == position, jnp.broadcast_to(row, (8, count)), out)
    return out


def build_list(fill, src_ref, tgt_ref, list_ref, column_leaves, half_id):
    slots = src_ref.shape[1]
    square = (slots, slots)
    id_row = (tgt_ref[...] * column_leaves + src_ref[...]).astype(F32)
    id_r = jnp.broadcast_to(id_row, square)
    id_c = id_r.T
    lane = lax.broadcasted_iota(jnp.int32, square, 1)
    sub = lax.broadcasted_iota(jnp.int32, square, 0)
    same = id_r == id_c
    ones = jnp.ones(square, BF16)

    def lane_sum(mask):
        return jnp.dot(mask.astype(F32).astype(BF16), ones, preferred_element_type=F32)

    count_c = lane_sum(same & (lane < fill))
    earlier_c = lane_sum(same & (lane < sub))
    first_c = (earlier_c == 0.0) & (sub < fill)
    earlier_r = jnp.sum(jnp.where(same & (sub < lane), 1.0, 0.0), axis=0, keepdims=True)
    first_r = (earlier_r == 0.0) & (lane[:1] < fill)
    rank_c = lane_sum(jnp.broadcast_to(jnp.where(first_r, 1.0, 0.0), square) * jnp.where(id_r < id_c, 1.0, 0.0) > 0.5)
    hit = first_c & (rank_c == lane.astype(F32))
    list_r = jnp.sum(jnp.where(hit, id_c, 0.0), axis=0, keepdims=True)
    copies_r = jnp.sum(jnp.where(hit, count_c, 0.0), axis=0, keepdims=True)
    total = jnp.sum(jnp.where(first_r, 1.0, 0.0))
    half = jnp.sum(jnp.where(first_r & (id_row < float(half_id)), 1.0, 0.0))
    index = lax.broadcasted_iota(jnp.int32, (8, slots), 0)
    table = jnp.where(index == 0, jnp.broadcast_to(list_r, (8, slots)), 0.0)
    table = jnp.where(index == 1, jnp.broadcast_to(copies_r, (8, slots)), table)
    table = jnp.where(index == 2, total, table)
    table = jnp.where(index == 3, half, table)
    list_ref[...] = table.astype(jnp.int32)


def entries_kernel(
    fill_ref, src_ref, tgt_ref, spts_ref, area_ref, tpts_ref,
    entries_ref, list_ref,
    s_ref, t_ref, table_ref, sem,
    *, column_leaves, row_leaves, leaf, unroll,
):
    fill = fill_ref[0, 0]
    build_list(fill, src_ref, tgt_ref, list_ref, column_leaves, (row_leaves // 2) * column_leaves)
    copy = pltpu.make_async_copy(list_ref, table_ref, sem)
    copy.start()

    tx, ty, tz = (tpts_ref[i : i + 1, :] - 0.5 for i in range(3))
    norm = tx * tx + ty * ty + tz * tz
    h1, h2, h3 = split3(feature_rows([tx, ty, tz, jnp.ones_like(tx), norm]))
    features = jnp.concatenate([h1, h2, h1, h2, h3, h1, jnp.zeros((16,) + h1.shape[1:], F32)], axis=0).astype(BF16)
    for t in range(row_leaves):
        t_ref[t] = features[:, t * leaf : (t + 1) * leaf]

    sx, sy, sz = (spts_ref[i : i + 1, :] - 0.5 for i in range(3))
    scale = area_ref[...] * INV_FOUR_PI
    weight = 1.0 / (scale * scale)
    norm = sx * sx + sy * sy + sz * sz + SOFTENING_SQ
    g1, g2, g3 = split3(
        feature_rows([-2.0 * weight * sx, -2.0 * weight * sy, -2.0 * weight * sz, weight * norm, weight])
    )
    features = jnp.concatenate([g1, g1, g2, g2, g1, g3, jnp.zeros((16,) + g1.shape[1:], F32)], axis=0)
    for s in range(column_leaves):
        s_ref[s] = features[:, s * leaf : (s + 1) * leaf].T.astype(BF16)

    copy.wait()
    total = table_ref[2, 0]

    @pl.loop(0, (total + unroll - 1) // unroll)
    def _(turn):
        for u in range(unroll):
            k = turn * unroll + u
            pair = table_ref[0, k]
            t = pair // column_leaves
            s = pair % column_leaves
            dist = jnp.dot(s_ref[s], t_ref[t], preferred_element_type=F32)
            entries_ref[k] = lax.rsqrt(dist).astype(BF16)


def make_entries(near_fill, near_source, near_target, source_points, source_areas, target_points, column_leaves, row_leaves):
    slots = near_source.shape[1]
    leaf = source_points.shape[1] // column_leaves
    depth = 64
    vmem = pl.BlockSpec(memory_space=pltpu.VMEM)
    smem = pl.BlockSpec(memory_space=pltpu.SMEM)
    return pl.pallas_call(
        functools.partial(
            entries_kernel, column_leaves=column_leaves, row_leaves=row_leaves, leaf=leaf, unroll=8
        ),
        out_shape=(
            pltpu.VMEM((slots, leaf, leaf), BF16),
            jax.ShapeDtypeStruct((8, slots), jnp.int32),
        ),
        in_specs=[smem, vmem, vmem, vmem, vmem, vmem],
        out_specs=(vmem, vmem),
        scratch_shapes=[
            pltpu.VMEM((column_leaves, leaf, depth), BF16),
            pltpu.VMEM((row_leaves, depth, leaf), BF16),
            pltpu.SMEM((8, slots), jnp.int32),
            pltpu.SemaphoreType.DMA,
        ],
        compiler_params=pltpu.CompilerParams(vmem_limit_bytes=16 << 20),
        cost_estimate=pl.CostEstimate(flops=8_000_000_000, bytes_accessed=1 << 20, transcendentals=0),
        name="entries",
    )(near_fill, near_source, near_target, source_points, source_areas[None, :], target_points)


def apply_kernel(*refs, pieces, plain, leaf, unroll):
    (table_ref, sfill_ref, tfill_ref, fsrc_ref, ftgt_ref, frank_ref, entries_ref, left_ref, right_ref) = refs[:9]
    piece_refs = refs[9 : 9 + pieces]
    x_ref, coef_ref, acc_ref = refs[-3:]
    out_refs = refs[9 + pieces : -3]
    column_leaves, rhs, _ = x_ref.shape
    row_leaves = acc_ref.shape[0]
    far_slots, rank, _ = left_ref.shape

    lane = lax.broadcasted_iota(jnp.int32, (rhs, leaf), 1)
    if not plain:
        parity = lax.rem(lax.axis_index("row"), 2)
    for s in range(column_leaves):
        window = slice(s * leaf, (s + 1) * leaf)
        if plain:
            block = piece_refs[0][:, window].astype(F32)
        else:
            rows = []
            for j in range(pieces // 2):
                mine = piece_refs[j][:, window].astype(F32)
                other = piece_refs[pieces // 2 + j][:, window].astype(F32)
                rows.append(jnp.where(parity == 0, mine, other))
                rows.append(jnp.where(parity == 0, other, mine))
            block = jnp.concatenate(rows, axis=0)
        x_ref[s] = jnp.where(lane < sfill_ref[s], block, 0.0).astype(BF16)

    acc_ref[...] = jnp.zeros_like(acc_ref)

    rank_lane = lax.broadcasted_iota(jnp.int32, (rhs, rank), 1)

    @pl.loop(0, far_slots // unroll)
    def _(turn):
        for u in range(unroll):
            k = turn * unroll + u
            coef = lax.dot_general(
                x_ref[fsrc_ref[0, k]], right_ref[k], (((1,), (1,)), ((), ())), preferred_element_type=F32
            )
            coef_ref[k] = jnp.where(rank_lane < frank_ref[0, k], coef, 0.0).astype(BF16)

    @pl.loop(0, far_slots // unroll)
    def _(turn):
        blocks = []
        for u in range(unroll):
            k = turn * unroll + u
            blocks.append(jnp.dot(coef_ref[k], left_ref[k], preferred_element_type=F32))
        for u in range(unroll):
            t = ftgt_ref[0, turn * unroll + u]
            acc_ref[t] = acc_ref[t] + blocks[u]

    total = table_ref[2, 0]

    @pl.loop(0, (total + unroll - 1) // unroll)
    def _(turn):
        blocks = []
        for u in range(unroll):
            k = turn * unroll + u
            blocks.append(
                jnp.dot(x_ref[table_ref[0, k] % column_leaves], entries_ref[k], preferred_element_type=F32)
            )
        for u in range(unroll):
            k = turn * unroll + u
            t = table_ref[0, k] // column_leaves
            copies = table_ref[1, k].astype(F32)
            acc_ref[t] = acc_ref[t] + jnp.where(copies > 0.0, blocks[u] * copies, 0.0)

    if plain:
        lane_t = lax.broadcasted_iota(jnp.int32, (rhs, leaf), 1)
        for t in range(row_leaves):
            out_refs[0][:, t * leaf : (t + 1) * leaf] = jnp.where(lane_t < tfill_ref[t], acc_ref[t], 0.0)
    else:
        owners = len(out_refs)
        height = rhs // owners
        lane_t = lax.broadcasted_iota(jnp.int32, (height, leaf), 1)
        base = lax.axis_index("col") ^ (lax.axis_index("row") // 2)
        for m in range(owners):
            start = pl.multiple_of((base ^ m) * height, height)
            for t in range(row_leaves):
                value = jnp.where(lane_t < tfill_ref[t], acc_ref[t, pl.ds(start, height), :], 0.0)
                out_refs[m][:, t * leaf : (t + 1) * leaf] = value.astype(out_refs[m].dtype)


def apply_blocks(table, source_fill, target_fill, far_source, far_target, far_rank, entries, left, right, pieces, owners, plain):
    column_leaves, row_leaves = source_fill.shape[0], target_fill.shape[0]
    far_slots, rank, leaf = left.shape
    rhs = sum(p.shape[0] for p in pieces)
    vmem = pl.BlockSpec(memory_space=pltpu.VMEM)
    smem = pl.BlockSpec(memory_space=pltpu.SMEM)
    width = row_leaves * leaf
    if plain:
        out_shape = (jax.ShapeDtypeStruct((rhs, width), F32),)
    else:
        out_shape = tuple(
            jax.ShapeDtypeStruct((rhs // owners, width), F32 if m == 0 else BF16) for m in range(owners)
        )
    return pl.pallas_call(
        functools.partial(apply_kernel, pieces=len(pieces), plain=plain, leaf=leaf, unroll=8),
        out_shape=out_shape,
        in_specs=[smem] * 6 + [vmem] * (3 + len(pieces)),
        out_specs=(vmem,) * len(out_shape),
        scratch_shapes=[
            pltpu.VMEM((column_leaves, rhs, leaf), BF16),
            pltpu.VMEM((far_slots, rhs, rank), BF16),
            pltpu.VMEM((row_leaves, rhs, leaf), F32),
        ],
        compiler_params=pltpu.CompilerParams(vmem_limit_bytes=16 << 20),
        cost_estimate=pl.CostEstimate(flops=8_000_000_000, bytes_accessed=8 << 20, transcendentals=0),
        name="apply",
    )(table, source_fill, target_fill, far_source, far_target, far_rank, entries, left, right, *pieces)


def shards(
    source_points, source_areas, source_fill, target_points, target_fill, charges, near_fill, near_source,
    near_target, far_source, far_target, far_rank, left_basis, right_basis, *, rows, columns,
):
    plain = charges.shape[0] % 8 != 0 or rows != 2 * columns
    if plain:
        pieces = [lax.all_gather(charges, "row", axis=0, tiled=True)]
    else:

        def swap(value, axis, size, mask):
            return lax.ppermute(value, axis, [(i, i ^ mask) for i in range(size)])

        pieces = [charges] + [swap(charges, "row", rows, mask) for mask in range(2, rows, 2)]
    entries, table = make_entries(
        near_fill, near_source, near_target, source_points, source_areas, target_points,
        source_fill.shape[0], target_fill.shape[0],
    )
    if not plain:
        pieces = pieces + [swap(piece, "row", rows, 1) for piece in pieces]
    outs = apply_blocks(
        table, source_fill, target_fill, far_source, far_target, far_rank, entries, left_basis[0], right_basis[0],
        pieces, columns, plain,
    )
    if plain:
        return lax.psum_scatter(outs[0], "col", scatter_dimension=0, tiled=True)
    result = outs[0]
    for mask in range(1, columns):
        result = result + swap(outs[mask], "col", columns, mask).astype(F32)
    return result


def solution(mesh):
    placed = (
        P(None, "col"), P("col"), P("col"), P(None, "row"), P("row"), P("row", "col"), P("row", "col"),
        P("row", "col"), P("row", "col"), P("row", "col"), P("row", "col"), P("row", "col"),
        P("row", "col", None, None), P("row", "col", None, None),
    )
    return jax.shard_map(
        functools.partial(shards, rows=mesh.shape["row"], columns=mesh.shape["col"]),
        mesh=mesh, in_specs=placed, out_specs=P("col", "row"), check_vma=False,
    )
```

profile of v0, /device:TPU:0, one launch (start us, length us, event | category | flops | bytes accessed | tf_op | source)
XLA Modules:
  0.0 77.2 jit_solution(751893856188155444)
XLA Ops:
  0.0 3.9 %collective-permute-start.2 = (bf16[8,8192]{1,0:T(8,128)(2,1)}, bf16[8,8192]{1,0:T(8,128)(2,1)S(1)}, u32[]{:S(2)}, u32[]{:S(2)}) collective-permute-start(bf16[8,8192]{1,0:T(8,128)(2,1)} %refs_9_.1), channel_id=1, source_target_pairs={{0,24},{4,28},{8,16},{12,20},{16,8},{20,12},{24,0},{28,4},{1,25},{... | collective-permute-start | bytes 393224 | tf_op jit(solution)/shard_map/ppermute | solution.py:257
  3.9 0.5 collective-permute-start.1
  4.4 0.1 collective-permute-start
  4.5 0.0 collective-permute-start.3
  5.1 3.0 %collective-permute-done.2.refs_12_ = bf16[8,8192]{1,0:T(8,128)(2,1)S(1)} collective-permute-done((bf16[8,8192]{1,0:T(8,128)(2,1)}, bf16[8,8192]{1,0:T(8,128)(2,1)S(1)}, u32[]{:S(2)}, u32[]{:S(2)}) %collective-permute-start.2) | collective-permute-done | bytes 131104 | tf_op jit(solution)/shard_map/ppermute | solution.py:257
  8.1 0.0 collective-permute-start.6
  8.1 2.3 %collective-permute-done.1.refs_11_ = bf16[8,8192]{1,0:T(8,128)(2,1)S(1)} collective-permute-done((bf16[8,8192]{1,0:T(8,128)(2,1)}, bf16[8,8192]{1,0:T(8,128)(2,1)S(1)}, u32[]{:S(2)}, u32[]{:S(2)}) %collective-permute-start.1) | collective-permute-done | bytes 131104 | tf_op jit(solution)/shard_map/ppermute | solution.py:257
  10.4 0.0 collective-permute-start.5
  10.4 0.2 collective-permute-done.refs_10_
  10.7 0.3 collective-permute-start.4
  11.0 0.0 copy-start.10
  11.0 0.9 %copy-done.10 = f32[3,8192]{1,0:T(4,128)S(1)} copy-done((f32[3,8192]{1,0:T(4,128)S(1)}, f32[3,8192]{1,0:T(4,128)}, u32[]{:S(2)}) %copy-start.10) | copy-done | bytes 98328
  11.9 0.0 copy-start.11
  11.9 0.8 %copy-done.11 = f32[3,4096]{1,0:T(4,128)S(1)} copy-done((f32[3,4096]{1,0:T(4,128)S(1)}, f32[3,4096]{1,0:T(4,128)}, u32[]{:S(2)}) %copy-start.11) | copy-done | bytes 49176
  12.7 0.0 copy-start.12
  12.7 0.8 copy-done.12
  13.5 0.0 copy-start.13
  13.5 0.7 copy-done.13
  14.1 0.7 copy-done.14
  14.8 0.0 copy-start.6
  14.8 0.0 copy-start.7
  14.8 0.0 copy-start.8
  14.9 0.0 copy-start.9
  14.9 12.5 %entries.1 = (bf16[256,256,256]{2,1,0:T(8,128)(2,1)S(1)}, s32[8,256]{1,0:T(8,128)S(1)}) custom-call(s32[1,1]{1,0:T(1,128)S(6)} %copy.15.fill_ref, s32[1,256]{1,0:T(1,128)S(1)} %copy-done.13, s32[1,256]{1,0:T(1,128)S(1)} %copy-done.14, f32[3,8192]{1,0:T(4,128)S(1)} %copy-done.10, f32[1,8192]{1,0:T(1,128)S(1)} %bitcast.5, f32[3,4096]{1,0:T(4,128)S(1)} %copy-done.11), custom_call_target="tpu_custom_call" | custom-call | flops 8000000000 | bytes 1048576 | tf_op jit(solution)/shard_map/entries/pallas_call | solution.py:115
  27.4 0.0 copy-start
  27.4 11.1 %copy-done = bf16[256,256,256]{2,1,0:T(8,128)(2,1)} copy-done((bf16[256,256,256]{2,1,0:T(8,128)(2,1)}, bf16[256,256,256]{2,1,0:T(8,128)(2,1)S(1)}, u32[]{:S(2)}) %copy-start) | copy-done | bytes 33554456
  38.5 0.0 collective-permute-done.3.refs_13_
  38.5 0.0 collective-permute-done.6.refs_16_
  38.5 0.0 collective-permute-done.5.refs_15_
  38.5 0.0 collective-permute-done.4.refs_14_
  38.5 0.0 copy-done.2
  38.5 0.0 copy-done.3
  38.5 0.0 copy-done.4
  38.5 0.0 copy-done.5
  38.5 0.0 copy-done.6
  38.6 0.0 copy-done.7
  38.6 0.0 copy-done.8
  38.6 0.0 copy-done.9
  38.6 0.0 copy-start.1
  38.6 10.5 %copy-done.1 = bf16[256,256,256]{2,1,0:T(8,128)(2,1)S(1)} copy-done((bf16[256,256,256]{2,1,0:T(8,128)(2,1)S(1)}, bf16[256,256,256]{2,1,0:T(8,128)(2,1)}, u32[]{:S(2)}) %copy-start.1) | copy-done | bytes 33554456
  49.1 14.2 %apply.1 = (f32[16,4096]{1,0:T(8,128)S(1)}, bf16[16,4096]{1,0:T(8,128)(2,1)S(1)}, bf16[16,4096]{1,0:T(8,128)(2,1)S(1)}, bf16[16,4096]{1,0:T(8,128)(2,1)S(1)}) custom-call(s32[8,256]{1,0:T(8,128)S(1)} %get-tuple-element.11.refs_0_, s32[32]{0:T(128)S(1)} %copy-done.5, s32[16]{0:T(128)S(1)} %copy-done.6, s32[1,96]{1,0:T(1,128)S(1)} %copy-done.7, ...), custom_call_target="tpu_custom_call" | custom-call | flops 8000000000 | bytes 8388608 | tf_op jit(solution)/shard_map/apply/pallas_call | solution.py:231
  63.4 0.1 collective-permute-start.7
  63.5 0.1 collective-permute-start.8
  63.5 4.3 %collective-permute-start.9 = (bf16[16,4096]{1,0:T(8,128)(2,1)S(1)}, bf16[16,4096]{1,0:T(8,128)(2,1)S(1)}, u32[]{:S(2)}, u32[]{:S(2)}) collective-permute-start(bf16[16,4096]{1,0:T(8,128)(2,1)S(1)} %get-tuple-element.16), channel_id=1, source_target_pairs={{0,3},{1,2},{2,1},{3,0},{4,7},{5,6},{6,5},{7,4},{8,11},{9,10},{10,... | collective-permute-start | bytes 393224 | tf_op jit(solution)/shard_map/ppermute | solution.py:257
  67.8 2.4 %collective-permute-done.7 = bf16[16,4096]{1,0:T(8,128)(2,1)S(1)} collective-permute-done((bf16[16,4096]{1,0:T(8,128)(2,1)S(1)}, bf16[16,4096]{1,0:T(8,128)(2,1)S(1)}, u32[]{:S(2)}, u32[]{:S(2)}) %collective-permute-start.7) | collective-permute-done | bytes 131104 | tf_op jit(solution)/shard_map/ppermute | solution.py:257
  70.2 6.2 %collective-permute-done.8 = bf16[16,4096]{1,0:T(8,128)(2,1)S(1)} collective-permute-done((bf16[16,4096]{1,0:T(8,128)(2,1)S(1)}, bf16[16,4096]{1,0:T(8,128)(2,1)S(1)}, u32[]{:S(2)}, u32[]{:S(2)}) %collective-permute-start.8) | collective-permute-done | bytes 131104 | tf_op jit(solution)/shard_map/ppermute | solution.py:257
  76.5 0.0 collective-permute-done.9
  76.5 0.8 convert_add_fusion
  (5 shorter events, 0.0 us)
Async XLA Ops:
  0.0 8.1 %collective-permute-start.2 = (bf16[8,8192]{1,0:T(8,128)(2,1)}, bf16[8,8192]{1,0:T(8,128)(2,1)S(1)}, u32[]{:S(2)}, u32[]{:S(2)}) collective-permute-start(bf16[8,8192]{1,0:T(8,128)(2,1)} %refs_9_.1), channel_id=1, source_target_pairs={{0,24},{4,28},{8,16},{12,20},{16,8},{20,12},{24,0},{28,4},{1,25},{... | collective-permute-start | bytes 393224 | tf_op jit(solution)/shard_map/ppermute | solution.py:257
  3.9 6.5 %collective-permute-start.1 = (bf16[8,8192]{1,0:T(8,128)(2,1)}, bf16[8,8192]{1,0:T(8,128)(2,1)S(1)}, u32[]{:S(2)}, u32[]{:S(2)}) collective-permute-start(bf16[8,8192]{1,0:T(8,128)(2,1)} %refs_9_.1), channel_id=1, source_target_pairs={{0,16},{4,20},{8,24},{12,28},{16,0},{20,4},{24,8},{28,12},{1,17},{... | collective-permute-start | bytes 393224 | tf_op jit(solution)/shard_map/ppermute | solution.py:257
  4.4 6.3 %collective-permute-start = (bf16[8,8192]{1,0:T(8,128)(2,1)}, bf16[8,8192]{1,0:T(8,128)(2,1)S(1)}, u32[]{:S(2)}, u32[]{:S(2)}) collective-permute-start(bf16[8,8192]{1,0:T(8,128)(2,1)} %refs_9_.1), channel_id=1, source_target_pairs={{0,8},{4,12},{8,0},{12,4},{16,24},{20,28},{24,16},{28,20},{1,9},{5... | collective-permute-start | bytes 393224 | tf_op jit(solution)/shard_map/ppermute | solution.py:257
  4.5 34.0 %collective-permute-start.3 = (bf16[8,8192]{1,0:T(8,128)(2,1)}, bf16[8,8192]{1,0:T(8,128)(2,1)S(1)}, u32[]{:S(2)}, u32[]{:S(2)}) collective-permute-start(bf16[8,8192]{1,0:T(8,128)(2,1)} %refs_9_.1), channel_id=1, source_target_pairs={{0,4},{4,0},{8,12},{12,8},{16,20},{20,16},{24,28},{28,24},{1,5},{5... | collective-permute-start | bytes 393224 | tf_op jit(solution)/shard_map/ppermute | solution.py:257
  8.1 30.4 %collective-permute-start.6 = (bf16[8,8192]{1,0:T(8,128)(2,1)S(1)}, bf16[8,8192]{1,0:T(8,128)(2,1)S(1)}, u32[]{:S(2)}, u32[]{:S(2)}) collective-permute-start(bf16[8,8192]{1,0:T(8,128)(2,1)S(1)} %collective-permute-done.2.refs_12_), channel_id=1, source_target_pairs={{0,4},{4,0},{8,12},{12,8},{16,20},{20,16},{24,28},{28,24},{1,5},{5... | collective-permute-start | bytes 393224 | tf_op jit(solution)/shard_map/ppermute | solution.py:257
  10.4 28.1 %collective-permute-start.5 = (bf16[8,8192]{1,0:T(8,128)(2,1)S(1)}, bf16[8,8192]{1,0:T(8,128)(2,1)S(1)}, u32[]{:S(2)}, u32[]{:S(2)}) collective-permute-start(bf16[8,8192]{1,0:T(8,128)(2,1)S(1)} %collective-permute-done.1.refs_11_), channel_id=1, source_target_pairs={{0,4},{4,0},{8,12},{12,8},{16,20},{20,16},{24,28},{28,24},{1,5},{5... | collective-permute-start | bytes 393224 | tf_op jit(solution)/shard_map/ppermute | solution.py:257
  10.7 27.8 %collective-permute-start.4 = (bf16[8,8192]{1,0:T(8,128)(2,1)S(1)}, bf16[8,8192]{1,0:T(8,128)(2,1)S(1)}, u32[]{:S(2)}, u32[]{:S(2)}) collective-permute-start(bf16[8,8192]{1,0:T(8,128)(2,1)S(1)} %collective-permute-done.refs_10_), channel_id=1, source_target_pairs={{0,4},{4,0},{8,12},{12,8},{16,20},{20,16},{24,28},{28,24},{1,5},{5... | collective-permute-start | bytes 393224 | tf_op jit(solution)/shard_map/ppermute | solution.py:257
  11.0 0.9 %copy-start.10 = (f32[3,8192]{1,0:T(4,128)S(1)}, f32[3,8192]{1,0:T(4,128)}, u32[]{:S(2)}) copy-start(f32[3,8192]{1,0:T(4,128)} %spts_ref.1) | copy-start | bytes 294916
  11.9 0.8 %copy-start.11 = (f32[3,4096]{1,0:T(4,128)S(1)}, f32[3,4096]{1,0:T(4,128)}, u32[]{:S(2)}) copy-start(f32[3,4096]{1,0:T(4,128)} %tpts_ref.1) | copy-start | bytes 147460
  12.7 0.8 copy-start.12
  13.5 0.7 copy-start.13
  14.1 0.7 copy-start.14
  14.8 23.7 %copy-start.2 = (bf16[1,96,32,256]{3,2,1,0:T(8,128)(2,1)S(1)}, bf16[1,96,32,256]{3,2,1,0:T(8,128)(2,1)}, u32[]{:S(2)}) copy-start(bf16[1,96,32,256]{3,2,1,0:T(8,128)(2,1)} %param.26) | copy-start | bytes 4718596
  14.8 23.7 %copy-start.3 = (bf16[1,96,32,256]{3,2,1,0:T(8,128)(2,1)S(1)}, bf16[1,96,32,256]{3,2,1,0:T(8,128)(2,1)}, u32[]{:S(2)}) copy-start(bf16[1,96,32,256]{3,2,1,0:T(8,128)(2,1)} %param.27) | copy-start | bytes 4718596
  14.8 23.7 %copy-start.4 = (bf16[8,8192]{1,0:T(8,128)(2,1)S(1)}, bf16[8,8192]{1,0:T(8,128)(2,1)}, u32[]{:S(2)}) copy-start(bf16[8,8192]{1,0:T(8,128)(2,1)} %refs_9_.1) | copy-start | bytes 393220
  14.8 23.7 %copy-start.5 = (s32[32]{0:T(128)S(1)}, s32[32]{0:T(128)}, u32[]{:S(2)}) copy-start(s32[32]{0:T(128)} %refs_1_.1) | copy-start | bytes 388
  14.8 23.7 %copy-start.6 = (s32[16]{0:T(128)S(1)}, s32[16]{0:T(128)}, u32[]{:S(2)}) copy-start(s32[16]{0:T(128)} %refs_2_.1) | copy-start | bytes 196
  14.8 23.7 %copy-start.7 = (s32[1,96]{1,0:T(1,128)S(1)}, s32[1,96]{1,0:T(1,128)}, u32[]{:S(2)}) copy-start(s32[1,96]{1,0:T(1,128)} %refs_3_.1) | copy-start | bytes 1156
  14.8 23.7 %copy-start.8 = (s32[1,96]{1,0:T(1,128)S(1)}, s32[1,96]{1,0:T(1,128)}, u32[]{:S(2)}) copy-start(s32[1,96]{1,0:T(1,128)} %refs_4_.1) | copy-start | bytes 1156
  14.9 23.7 %copy-start.9 = (s32[1,96]{1,0:T(1,128)S(1)}, s32[1,96]{1,0:T(1,128)}, u32[]{:S(2)}) copy-start(s32[1,96]{1,0:T(1,128)} %refs_5_.1) | copy-start | bytes 1156
  27.4 11.1 %copy-start = (bf16[256,256,256]{2,1,0:T(8,128)(2,1)}, bf16[256,256,256]{2,1,0:T(8,128)(2,1)S(1)}, u32[]{:S(2)}) copy-start(bf16[256,256,256]{2,1,0:T(8,128)(2,1)S(1)} %get-tuple-element.12.refs_6_) | copy-start | bytes 100663296
  38.6 10.5 %copy-start.1 = (bf16[256,256,256]{2,1,0:T(8,128)(2,1)S(1)}, bf16[256,256,256]{2,1,0:T(8,128)(2,1)}, u32[]{:S(2)}) copy-start(bf16[256,256,256]{2,1,0:T(8,128)(2,1)} %copy-done) | copy-start | bytes 100663296
  63.4 6.9 %collective-permute-start.7 = (bf16[16,4096]{1,0:T(8,128)(2,1)S(1)}, bf16[16,4096]{1,0:T(8,128)(2,1)S(1)}, u32[]{:S(2)}, u32[]{:S(2)}) collective-permute-start(bf16[16,4096]{1,0:T(8,128)(2,1)S(1)} %get-tuple-element.14), channel_id=1, source_target_pairs={{0,1},{1,0},{2,3},{3,2},{4,5},{5,4},{6,7},{7,6},{8,9},{9,8},{10,11... | collective-permute-start | bytes 393224 | tf_op jit(solution)/shard_map/ppermute | solution.py:257
  63.5 13.0 %collective-permute-start.8 = (bf16[16,4096]{1,0:T(8,128)(2,1)S(1)}, bf16[16,4096]{1,0:T(8,128)(2,1)S(1)}, u32[]{:S(2)}, u32[]{:S(2)}) collective-permute-start(bf16[16,4096]{1,0:T(8,128)(2,1)S(1)} %get-tuple-element.15), channel_id=1, source_target_pairs={{0,2},{1,3},{2,0},{3,1},{4,6},{5,7},{6,4},{7,5},{8,10},{9,11},{10,... | collective-permute-start | bytes 393224 | tf_op jit(solution)/shard_map/ppermute | solution.py:257
  63.5 12.9 %collective-permute-start.9 = (bf16[16,4096]{1,0:T(8,128)(2,1)S(1)}, bf16[16,4096]{1,0:T(8,128)(2,1)S(1)}, u32[]{:S(2)}, u32[]{:S(2)}) collective-permute-start(bf16[16,4096]{1,0:T(8,128)(2,1)S(1)} %get-tuple-element.16), channel_id=1, source_target_pairs={{0,3},{1,2},{2,1},{3,0},{4,7},{5,6},{6,5},{7,4},{8,11},{9,10},{10,... | collective-permute-start | bytes 393224 | tf_op jit(solution)/shard_map/ppermute | solution.py:257
where the time goes:
time: 78.4 us; the launch traced here: 77.2 us
  Pallas kernels  26.8 us (34%)
  local copies, waits for them, and re-layouts  25.5 us (33%)
  waiting for transfers between devices  14.2 us (18%)
  starting transfers between devices  9.2 us (12%)
  between operations  0.82 us (1%)
    unnamed x30, local copies, waits for them, and re-layouts  25.5 us
    pallas_call x1, Pallas kernels, apply_blocks(): pl.pallas_call(functools.partial(apply_kernel, pieces=len(pieces), plain=...  14.2 us
    ppermute x10, waiting for transfers between devices, swap(): return lax.ppermute(value, axis, [(i, i ^ mask) for i in range(size)])  14.2 us
    pallas_call x1, Pallas kernels, make_entries(): pl.pallas_call(functools.partial(entries_kernel, column_leaves=column_lea...  12.5 us
    ppermute x10, starting transfers between devices, swap(): return lax.ppermute(value, axis, [(i, i ^ mask) for i in range(size)])  9.2 us
  transfers between devices with their start and end apart: 10, of which 5 were waited for; matrix products, arithmetic and copies ran while one was open for 0% of the time, Pallas kernels for 16%

commit v1 on v0

--- a/solution.py
+++ b/solution.py
@@ -28,6 +28,10 @@
     for position, row in enumerate(rows):
         out = jnp.where(index == position, jnp.broadcast_to(row, (8, count)), out)
     return out
+
+
+def part_count(slots):
+    return 4 if slots % 32 == 0 else 1
 
 
 def build_list(fill, src_ref, tgt_ref, list_ref, column_leaves, half_id):
@@ -63,16 +67,22 @@
     list_ref[...] = table.astype(jnp.int32)
 
 
-def entries_kernel(
-    fill_ref, src_ref, tgt_ref, spts_ref, area_ref, tpts_ref,
-    entries_ref, list_ref,
-    s_ref, t_ref, table_ref, sem,
-    *, column_leaves, row_leaves, leaf, unroll,
-):
+def entries_kernel(*refs, column_leaves, row_leaves, leaf, parts, unroll):
+    inputs, outputs, scratch = refs[:6], refs[6 : 7 + parts], refs[7 + parts :]
+    entries_refs, list_ref = outputs[:-1], outputs[-1]
+    copies, (s_ref, t_ref, table_ref, sem, in_sem) = scratch[:6], scratch[6:]
+    loads = [pltpu.make_async_copy(src, dst, in_sem.at[i]) for i, (src, dst) in enumerate(zip(inputs, copies))]
+    for load in loads:
+        load.start()
+    fill_ref, src_ref, tgt_ref, spts_ref, area_ref, tpts_ref = copies
+    for load in loads[:3]:
+        load.wait()
     fill = fill_ref[0, 0]
     build_list(fill, src_ref, tgt_ref, list_ref, column_leaves, (row_leaves // 2) * column_leaves)
     copy = pltpu.make_async_copy(list_ref, table_ref, sem)
     copy.start()
+    for load in loads[3:]:
+        load.wait()
 
     tx, ty, tz = (tpts_ref[i : i + 1, :] - 0.5 for i in range(3))
     norm = tx * tx + ty * ty + tz * tz
@@ -95,15 +105,19 @@
     copy.wait()
     total = table_ref[2, 0]
 
-    @pl.loop(0, (total + unroll - 1) // unroll)
-    def _(turn):
-        for u in range(unroll):
-            k = turn * unroll + u
-            pair = table_ref[0, k]
-            t = pair // column_leaves
-            s = pair % column_leaves
-            dist = jnp.dot(s_ref[s], t_ref[t], preferred_element_type=F32)
-            entries_ref[k] = lax.rsqrt(dist).astype(BF16)
+    for part, entries_ref in enumerate(entries_refs):
+        size = entries_ref.shape[0]
+        count = jnp.clip(total - part * size, 0, size)
+
+        @pl.loop(0, (count + unroll - 1) // unroll)
+        def _(turn):
+            for u in range(unroll):
+                k = turn * unroll + u
+                pair = table_ref[0, part * size + k]
+                t = pair // column_leaves
+                s = pair % column_leaves
+                dist = jnp.dot(s_ref[s], t_ref[t], preferred_element_type=F32)
+                entries_ref[k] = lax.rsqrt(dist).astype(BF16)
 
 
 def make_entries(near_fill, near_source, near_target, source_points, source_areas, target_points, column_leaves, row_leaves):
@@ -111,34 +125,38 @@
     leaf = source_points.shape[1] // column_leaves
     depth = 64
     vmem = pl.BlockSpec(memory_space=pltpu.VMEM)
-    smem = pl.BlockSpec(memory_space=pltpu.SMEM)
+    hbm = pl.BlockSpec(memory_space=pltpu.HBM)
+    parts = part_count(slots)
+    inputs = (near_fill, near_source, near_target, source_points, source_areas[None, :], target_points)
     return pl.pallas_call(
         functools.partial(
-            entries_kernel, column_leaves=column_leaves, row_leaves=row_leaves, leaf=leaf, unroll=8
+            entries_kernel, column_leaves=column_leaves, row_leaves=row_leaves, leaf=leaf, parts=parts, unroll=8
         ),
-        out_shape=(
-            pltpu.VMEM((slots, leaf, leaf), BF16),
-            jax.ShapeDtypeStruct((8, slots), jnp.int32),
-        ),
-        in_specs=[smem, vmem, vmem, vmem, vmem, vmem],
-        out_specs=(vmem, vmem),
-        scratch_shapes=[
+        out_shape=(pltpu.VMEM((slots // parts, leaf, leaf), BF16),) * parts
+        + (jax.ShapeDtypeStruct((8, slots), jnp.int32),),
+        in_specs=[hbm] * len(inputs),
+        out_specs=(vmem,) * (parts + 1),
+        scratch_shapes=[pltpu.SMEM((1, 1), jnp.int32)]
+        + [pltpu.VMEM(value.shape, value.dtype) for value in inputs[1:]]
+        + [
             pltpu.VMEM((column_leaves, leaf, depth), BF16),
             pltpu.VMEM((row_leaves, depth, leaf), BF16),
             pltpu.SMEM((8, slots), jnp.int32),
             pltpu.SemaphoreType.DMA,
+            pltpu.SemaphoreType.DMA((len(inputs),)),
         ],
         compiler_params=pltpu.CompilerParams(vmem_limit_bytes=16 << 20),
         cost_estimate=pl.CostEstimate(flops=8_000_000_000, bytes_accessed=1 << 20, transcendentals=0),
         name="entries",
-    )(near_fill, near_source, near_target, source_points, source_areas[None, :], target_points)
-
-
-def apply_kernel(*refs, pieces, plain, leaf, unroll):
-    (table_ref, sfill_ref, tfill_ref, fsrc_ref, ftgt_ref, frank_ref, entries_ref, left_ref, right_ref) = refs[:9]
-    piece_refs = refs[9 : 9 + pieces]
+    )(*inputs)
+
+
+def apply_kernel(*refs, pieces, parts, plain, leaf, unroll):
+    (table_ref, sfill_ref, tfill_ref, fsrc_ref, ftgt_ref, frank_ref, left_ref, right_ref) = refs[:8]
+    piece_refs = refs[8 : 8 + pieces]
+    entries_refs = refs[8 + pieces : 8 + pieces + parts]
     x_ref, coef_ref, acc_ref = refs[-3:]
-    out_refs = refs[9 + pieces : -3]
+    out_refs = refs[8 + pieces + parts : -3]
     column_leaves, rhs, _ = x_ref.shape
     row_leaves = acc_ref.shape[0]
     far_slots, rank, _ = left_ref.shape
@@ -185,19 +203,22 @@
 
     total = table_ref[2, 0]
 
-    @pl.loop(0, (total + unroll - 1) // unroll)
-    def _(turn):
-        blocks = []
-        for u in range(unroll):
-            k = turn * unroll + u
-            blocks.append(
-                jnp.dot(x_ref[table_ref[0, k] % column_leaves], entries_ref[k], preferred_element_type=F32)
-            )
-        for u in range(unroll):
-            k = turn * unroll + u
-            t = table_ref[0, k] // column_leaves
-            copies = table_ref[1, k].astype(F32)
-            acc_ref[t] = acc_ref[t] + jnp.where(copies > 0.0, blocks[u] * copies, 0.0)
+    for part, entries_ref in enumerate(entries_refs):
+        size = entries_ref.shape[0]
+        count = jnp.clip(total - part * size, 0, size)
+
+        @pl.loop(0, (count + unroll - 1) // unroll)
+        def _(turn):
+            blocks = []
+            for u in range(unroll):
+                k = turn * unroll + u
+                source = table_ref[0, part * size + k] % column_leaves
+                blocks.append(jnp.dot(x_ref[source], entries_ref[k], preferred_element_type=F32))
+            for u in range(unroll):
+                k = part * size + turn * unroll + u
+                t = table_ref[0, k] // column_leaves
+                copies = table_ref[1, k].astype(F32)
+                acc_ref[t] = acc_ref[t] + jnp.where(copies > 0.0, blocks[u] * copies, 0.0)
 
     if plain:
         lane_t = lax.broadcasted_iota(jnp.int32, (rhs, leaf), 1)
@@ -229,9 +250,9 @@
             jax.ShapeDtypeStruct((rhs // owners, width), F32 if m == 0 else BF16) for m in range(owners)
         )
     return pl.pallas_call(
-        functools.partial(apply_kernel, pieces=len(pieces), plain=plain, leaf=leaf, unroll=8),
+        functools.partial(apply_kernel, pieces=len(pieces), parts=len(entries), plain=plain, leaf=leaf, unroll=8),
         out_shape=out_shape,
-        in_specs=[smem] * 6 + [vmem] * (3 + len(pieces)),
+        in_specs=[smem] * 6 + [vmem] * (2 + len(pieces) + len(entries)),
         out_specs=(vmem,) * len(out_shape),
         scratch_shapes=[
             pltpu.VMEM((column_leaves, rhs, leaf), BF16),
@@ -241,7 +262,7 @@
         compiler_params=pltpu.CompilerParams(vmem_limit_bytes=16 << 20),
         cost_estimate=pl.CostEstimate(flops=8_000_000_000, bytes_accessed=8 << 20, transcendentals=0),
         name="apply",
-    )(table, source_fill, target_fill, far_source, far_target, far_rank, entries, left, right, *pieces)
+    )(table, source_fill, target_fill, far_source, far_target, far_rank, left, right, *pieces, *entries)
 
 
 def shards(
@@ -257,11 +278,12 @@
             return lax.ppermute(value, axis, [(i, i ^ mask) for i in range(size)])
 
         pieces = [charges] + [swap(charges, "row", rows, mask) for mask in range(2, rows, 2)]
-    entries, table = make_entries(
+    *entries, table = make_entries(
         near_fill, near_source, near_target, source_points, source_areas, target_points,
         source_fill.shape[0], target_fill.shape[0],
     )
     if not plain:
+        pieces, table = lax.optimization_barrier((pieces, table))
         pieces = pieces + [swap(piece, "row", rows, 1) for piece in pieces]
     outs = apply_blocks(
         table, source_fill, target_fill, far_source, far_target, far_rank, entries, left_basis[0], right_basis[0],
@@ -270,7 +292,7 @@
     if plain:
         return lax.psum_scatter(outs[0], "col", scatter_dimension=0, tiled=True)
     result = outs[0]
-    for mask in range(1, columns):
+    for mask in reversed(range(1, columns)):
         result = result + swap(outs[mask], "col", columns, mask).astype(F32)
     return result
 

time: 78.4 us -> 52.1 us (0.66); the launches traced: 77.2 us -> 51.9 us
  local copies, waits for them, and re-layouts: 25.5 us -> 3.89 us
  waiting for transfers between devices: 14.2 us -> 9.01 us
  starting transfers between devices: 9.2 us -> 10 us
    unnamed x30 -> x26, local copies, waits for them, and re-layouts: 25.5 us -> 3.89 us
    ppermute x10, waiting for transfers between devices: 14.2 us -> 9.01 us  [swap(): return lax.ppermute(value, axis, [(i, i ^ mask) for i in range(size)])]
    ppermute x10, starting transfers between devices: 9.2 us -> 10 us  [swap(): return lax.ppermute(value, axis, [(i, i ^ mask) for i in range(size)])]
  transfers between devices with their start and end apart: 10 -> 10, of which waited for: 5 -> 6; matrix products, arithmetic and copies ran while one was open for 0% -> 0% of each run, Pallas kernels for 16% -> 25%
where the time goes in v1:
time: 52.1 us; the launch traced here: 51.9 us
  Pallas kernels  27.4 us (53%)
  starting transfers between devices  10 us (19%)
  waiting for transfers between devices  9.01 us (17%)
  local copies, waits for them, and re-layouts  3.89 us (7%)
  between operations  0.81 us (2%)
  other arithmetic  0.77 us (1%)
    pallas_call x1, Pallas kernels, apply_blocks(): pl.pallas_call(functools.partial(apply_kernel, pieces=len(pieces), parts=...  14.5 us
    pallas_call x1, Pallas kernels, make_entries(): pl.pallas_call(functools.partial(entries_kernel, column_leaves=column_lea...  13 us
    ppermute x10, starting transfers between devices, swap(): return lax.ppermute(value, axis, [(i, i ^ mask) for i in range(size)])  10 us
    ppermute x10, waiting for transfers between devices, swap(): return lax.ppermute(value, axis, [(i, i ^ mask) for i in range(size)])  9.01 us
    unnamed x26, local copies, waits for them, and re-layouts  3.89 us
  transfers between devices with their start and end apart: 10, of which 6 were waited for; matrix products, arithmetic and copies ran while one was open for 0% of the time, Pallas kernels for 25%

profile of v1, /device:TPU:0, one launch (start us, length us, event | category | flops | bytes accessed | tf_op | source)
XLA Modules:
  0.0 51.9 jit_solution(1407020325466910985)
XLA Ops:
  0.0 3.0 %collective-permute-start.1 = (bf16[8,8192]{1,0:T(8,128)(2,1)}, bf16[8,8192]{1,0:T(8,128)(2,1)S(1)}, u32[]{:S(2)}, u32[]{:S(2)}) collective-permute-start(bf16[8,8192]{1,0:T(8,128)(2,1)} %refs_8_), channel_id=1, source_target_pairs={{0,16},{4,20},{8,24},{12,28},{16,0},{20,4},{24,8},{28,12},{1,17},{... | collective-permute-start | bytes 393224 | tf_op jit(solution)/shard_map/ppermute | solution.py:278
  3.0 1.5 %collective-permute-start = (bf16[8,8192]{1,0:T(8,128)(2,1)}, bf16[8,8192]{1,0:T(8,128)(2,1)S(1)}, u32[]{:S(2)}, u32[]{:S(2)}) collective-permute-start(bf16[8,8192]{1,0:T(8,128)(2,1)} %refs_8_), channel_id=1, source_target_pairs={{0,8},{4,12},{8,0},{12,4},{16,24},{20,28},{24,16},{28,20},{1,9},{5... | collective-permute-start | bytes 393224 | tf_op jit(solution)/shard_map/ppermute | solution.py:278
  4.5 0.0 collective-permute-start.2
  5.1 0.0 copy-start.8
  5.2 0.9 %copy-done.8 = f32[3,8192]{1,0:T(4,128)S(1)} copy-done((f32[3,8192]{1,0:T(4,128)S(1)}, f32[3,8192]{1,0:T(4,128)}, u32[]{:S(2)}) %copy-start.8) | copy-done | bytes 98328
  6.0 0.0 copy-start.9
  6.1 0.8 %copy-done.9 = f32[3,4096]{1,0:T(4,128)S(1)} copy-done((f32[3,4096]{1,0:T(4,128)S(1)}, f32[3,4096]{1,0:T(4,128)}, u32[]{:S(2)}) %copy-start.9) | copy-done | bytes 49176
  6.9 0.0 copy-start.10
  6.9 0.8 %copy-done.10 = f32[8192]{0:T(1024)S(1)} copy-done((f32[8192]{0:T(1024)S(1)}, f32[8192]{0:T(1024)}, u32[]{:S(2)}) %copy-start.10) | copy-done | bytes 32792
  7.6 0.0 copy-start.11
  7.6 0.7 %copy-done.11 = s32[1,256]{1,0:T(1,128)S(1)} copy-done((s32[1,256]{1,0:T(1,128)S(1)}, s32[1,256]{1,0:T(1,128)}, u32[]{:S(2)}) %copy-start.11) | copy-done | bytes 1048
  8.3 0.0 copy-start.12
  8.3 0.7 %copy-done.12 = s32[1,256]{1,0:T(1,128)S(1)} copy-done((s32[1,256]{1,0:T(1,128)S(1)}, s32[1,256]{1,0:T(1,128)}, u32[]{:S(2)}) %copy-start.12) | copy-done | bytes 1048
  9.0 0.0 copy-start.2
  9.0 0.0 copy-start
  9.0 0.0 copy-start.1
  9.0 0.0 copy-start.4
  9.0 0.0 copy-start.5
  9.0 0.0 copy-start.6
  9.1 0.0 copy-start.7
  9.1 13.0 %entries.1 = (bf16[64,256,256]{2,1,0:T(8,128)(2,1)S(1)}, bf16[64,256,256]{2,1,0:T(8,128)(2,1)S(1)}, bf16[64,256,256]{2,1,0:T(8,128)(2,1)S(1)}, bf16[64,256,256]{2,1,0:T(8,128)(2,1)S(1)}, s32[8,256]{1,0:T(8,128)S(1)}) custom-call(s32[1,1]{1,0:T(1,128)S(6)} %copy.15.refs_0_, s32[1,256]{1,0:T(1,128)S(1)} %copy-done.11, s32[1,256]{1,0:T(1,128)S(1)} %copy-done.12, ...), custom_call_target="tpu_custom_call" | custom-call | flops 8000000000 | bytes 1048576 | tf_op jit(solution)/shard_map/entries/pallas_call | solution.py:131
  22.0 0.0 collective-permute-done.1.refs_10_
  22.1 0.0 collective-permute-done.refs_9_
  22.1 0.0 collective-permute-done.2.refs_11_
  22.1 0.0 copy-done.2
  22.1 0.1 collective-permute-start.3
  22.2 0.5 collective-permute-start.4
  22.7 0.1 collective-permute-start.5
  22.7 0.4 collective-permute-start.6
  23.2 0.3 collective-permute-done.3.refs_12_
  23.5 0.2 collective-permute-done.4.refs_13_
  23.7 0.3 collective-permute-done.5.refs_14_
  24.0 0.2 collective-permute-done.6.refs_15_
  24.2 0.0 copy-done
  24.2 0.0 copy-done.1
  24.2 0.0 copy-done.3
  24.2 0.0 copy-done.4
  24.2 0.0 copy-done.5
  24.2 0.0 copy-done.6
  24.2 0.0 copy-done.7
  24.3 14.5 %apply.1 = (f32[16,4096]{1,0:T(8,128)S(1)}, bf16[16,4096]{1,0:T(8,128)(2,1)S(1)}, bf16[16,4096]{1,0:T(8,128)(2,1)S(1)}, bf16[16,4096]{1,0:T(8,128)(2,1)S(1)}) custom-call(s32[8,256]{1,0:T(8,128)S(1)} %get-tuple-element.20.refs_0_, s32[32]{0:T(128)S(1)} %copy-done.3, s32[16]{0:T(128)S(1)} %copy-done.4, s32[1,96]{1,0:T(1,128)S(1)} %copy-done.5, ...), custom_call_target="tpu_custom_call" | custom-call | flops 8000000000 | bytes 8388608 | tf_op jit(solution)/shard_map/apply/pallas_call | solution.py:252
  38.7 0.1 collective-permute-start.7
  38.8 0.1 collective-permute-start.8
  38.9 4.3 %collective-permute-start.9 = (bf16[16,4096]{1,0:T(8,128)(2,1)S(1)}, bf16[16,4096]{1,0:T(8,128)(2,1)S(1)}, u32[]{:S(2)}, u32[]{:S(2)}) collective-permute-start(bf16[16,4096]{1,0:T(8,128)(2,1)S(1)} %get-tuple-element.32), channel_id=1, source_target_pairs={{0,1},{1,0},{2,3},{3,2},{4,5},{5,4},{6,7},{7,6},{8,9},{9,8},{10,11... | collective-permute-start | bytes 393224 | tf_op jit(solution)/shard_map/ppermute | solution.py:278
  43.2 3.9 %collective-permute-done.7 = bf16[16,4096]{1,0:T(8,128)(2,1)S(1)} collective-permute-done((bf16[16,4096]{1,0:T(8,128)(2,1)S(1)}, bf16[16,4096]{1,0:T(8,128)(2,1)S(1)}, u32[]{:S(2)}, u32[]{:S(2)}) %collective-permute-start.7) | collective-permute-done | bytes 131104 | tf_op jit(solution)/shard_map/ppermute | solution.py:278
  47.1 4.1 %collective-permute-done.8 = bf16[16,4096]{1,0:T(8,128)(2,1)S(1)} collective-permute-done((bf16[16,4096]{1,0:T(8,128)(2,1)S(1)}, bf16[16,4096]{1,0:T(8,128)(2,1)S(1)}, u32[]{:S(2)}, u32[]{:S(2)}) %collective-permute-start.8) | collective-permute-done | bytes 131104 | tf_op jit(solution)/shard_map/ppermute | solution.py:278
  51.1 0.0 collective-permute-done.9
  51.1 0.8 %convert_add_fusion = f32[16,4096]{1,0:T(8,128)} fusion(bf16[16,4096]{1,0:T(8,128)(2,1)S(1)} %collective-permute-done.9, bf16[16,4096]{1,0:T(8,128)(2,1)S(1)} %collective-permute-done.8, f32[16,4096]{1,0:T(8,128)S(1)} %get-tuple-element.29, bf16[16,4096]{1,0:T(8,128)(2,1)S(1)} %collective-permute-done.7), kind=kLoop, calls=%fused_computation | loop fusion | flops 393216 | bytes 917504 | tf_op jit(solution)/shard_map/add | solution.py:296
  (1 shorter events, 0.0 us)
Async XLA Ops:
  0.0 22.0 %collective-permute-start.1 = (bf16[8,8192]{1,0:T(8,128)(2,1)}, bf16[8,8192]{1,0:T(8,128)(2,1)S(1)}, u32[]{:S(2)}, u32[]{:S(2)}) collective-permute-start(bf16[8,8192]{1,0:T(8,128)(2,1)} %refs_8_), channel_id=1, source_target_pairs={{0,16},{4,20},{8,24},{12,28},{16,0},{20,4},{24,8},{28,12},{1,17},{... | collective-permute-start | bytes 393224 | tf_op jit(solution)/shard_map/ppermute | solution.py:278
  3.0 19.1 %collective-permute-start = (bf16[8,8192]{1,0:T(8,128)(2,1)}, bf16[8,8192]{1,0:T(8,128)(2,1)S(1)}, u32[]{:S(2)}, u32[]{:S(2)}) collective-permute-start(bf16[8,8192]{1,0:T(8,128)(2,1)} %refs_8_), channel_id=1, source_target_pairs={{0,8},{4,12},{8,0},{12,4},{16,24},{20,28},{24,16},{28,20},{1,9},{5... | collective-permute-start | bytes 393224 | tf_op jit(solution)/shard_map/ppermute | solution.py:278
  4.5 17.6 %collective-permute-start.2 = (bf16[8,8192]{1,0:T(8,128)(2,1)}, bf16[8,8192]{1,0:T(8,128)(2,1)S(1)}, u32[]{:S(2)}, u32[]{:S(2)}) collective-permute-start(bf16[8,8192]{1,0:T(8,128)(2,1)} %refs_8_), channel_id=1, source_target_pairs={{0,24},{4,28},{8,16},{12,20},{16,8},{20,12},{24,0},{28,4},{1,25},{... | collective-permute-start | bytes 393224 | tf_op jit(solution)/shard_map/ppermute | solution.py:278
  5.1 0.9 %copy-start.8 = (f32[3,8192]{1,0:T(4,128)S(1)}, f32[3,8192]{1,0:T(4,128)}, u32[]{:S(2)}) copy-start(f32[3,8192]{1,0:T(4,128)} %refs_3_.2) | copy-start | bytes 294916
  6.0 0.8 %copy-start.9 = (f32[3,4096]{1,0:T(4,128)S(1)}, f32[3,4096]{1,0:T(4,128)}, u32[]{:S(2)}) copy-start(f32[3,4096]{1,0:T(4,128)} %refs_5_.2) | copy-start | bytes 147460
  6.9 0.8 %copy-start.10 = (f32[8192]{0:T(1024)S(1)}, f32[8192]{0:T(1024)}, u32[]{:S(2)}) copy-start(f32[8192]{0:T(1024)} %param.15) | copy-start | bytes 98308
  7.6 0.7 %copy-start.11 = (s32[1,256]{1,0:T(1,128)S(1)}, s32[1,256]{1,0:T(1,128)}, u32[]{:S(2)}) copy-start(s32[1,256]{1,0:T(1,128)} %refs_1_.2) | copy-start | bytes 3076
  8.3 0.7 %copy-start.12 = (s32[1,256]{1,0:T(1,128)S(1)}, s32[1,256]{1,0:T(1,128)}, u32[]{:S(2)}) copy-start(s32[1,256]{1,0:T(1,128)} %refs_2_.2) | copy-start | bytes 3076
  9.0 13.1 %copy-start.2 = (bf16[8,8192]{1,0:T(8,128)(2,1)S(1)}, bf16[8,8192]{1,0:T(8,128)(2,1)}, u32[]{:S(2)}) copy-start(bf16[8,8192]{1,0:T(8,128)(2,1)} %refs_8_) | copy-start | bytes 393220
  9.0 15.2 %copy-start = (bf16[1,96,32,256]{3,2,1,0:T(8,128)(2,1)S(1)}, bf16[1,96,32,256]{3,2,1,0:T(8,128)(2,1)}, u32[]{:S(2)}) copy-start(bf16[1,96,32,256]{3,2,1,0:T(8,128)(2,1)} %param.26) | copy-start | bytes 4718596
  9.0 15.2 %copy-start.1 = (bf16[1,96,32,256]{3,2,1,0:T(8,128)(2,1)S(1)}, bf16[1,96,32,256]{3,2,1,0:T(8,128)(2,1)}, u32[]{:S(2)}) copy-start(bf16[1,96,32,256]{3,2,1,0:T(8,128)(2,1)} %param.27) | copy-start | bytes 4718596
  9.0 15.2 %copy-start.3 = (s32[32]{0:T(128)S(1)}, s32[32]{0:T(128)}, u32[]{:S(2)}) copy-start(s32[32]{0:T(128)} %refs_1_.3) | copy-start | bytes 388
  9.0 15.2 %copy-start.4 = (s32[16]{0:T(128)S(1)}, s32[16]{0:T(128)}, u32[]{:S(2)}) copy-start(s32[16]{0:T(128)} %refs_2_.3) | copy-start | bytes 196
  9.0 15.2 %copy-start.5 = (s32[1,96]{1,0:T(1,128)S(1)}, s32[1,96]{1,0:T(1,128)}, u32[]{:S(2)}) copy-start(s32[1,96]{1,0:T(1,128)} %refs_3_.3) | copy-start | bytes 1156
  9.0 15.2 %copy-start.6 = (s32[1,96]{1,0:T(1,128)S(1)}, s32[1,96]{1,0:T(1,128)}, u32[]{:S(2)}) copy-start(s32[1,96]{1,0:T(1,128)} %refs_4_.1) | copy-start | bytes 1156
  9.1 15.2 %copy-start.7 = (s32[1,96]{1,0:T(1,128)S(1)}, s32[1,96]{1,0:T(1,128)}, u32[]{:S(2)}) copy-start(s32[1,96]{1,0:T(1,128)} %refs_5_.3) | copy-start | bytes 1156
  22.1 1.4 %collective-permute-start.3 = (bf16[8,8192]{1,0:T(8,128)(2,1)S(1)}, bf16[8,8192]{1,0:T(8,128)(2,1)S(1)}, u32[]{:S(2)}, u32[]{:S(2)}) collective-permute-start(bf16[8,8192]{1,0:T(8,128)(2,1)S(1)} %copy-done.2), channel_id=1, source_target_pairs={{0,4},{4,0},{8,12},{12,8},{16,20},{20,16},{24,28},{28,24},{1,5},{5... | collective-permute-start | bytes 393224 | tf_op jit(solution)/shard_map/ppermute | solution.py:278
  22.2 1.5 %collective-permute-start.4 = (bf16[8,8192]{1,0:T(8,128)(2,1)S(1)}, bf16[8,8192]{1,0:T(8,128)(2,1)S(1)}, u32[]{:S(2)}, u32[]{:S(2)}) collective-permute-start(bf16[8,8192]{1,0:T(8,128)(2,1)S(1)} %collective-permute-done.refs_9_), channel_id=1, source_target_pairs={{0,4},{4,0},{8,12},{12,8},{16,20},{20,16},{24,28},{28,24},{1,5},{5... | collective-permute-start | bytes 393224 | tf_op jit(solution)/shard_map/ppermute | solution.py:278
  22.7 1.3 %collective-permute-start.5 = (bf16[8,8192]{1,0:T(8,128)(2,1)S(1)}, bf16[8,8192]{1,0:T(8,128)(2,1)S(1)}, u32[]{:S(2)}, u32[]{:S(2)}) collective-permute-start(bf16[8,8192]{1,0:T(8,128)(2,1)S(1)} %collective-permute-done.1.refs_10_), channel_id=1, source_target_pairs={{0,4},{4,0},{8,12},{12,8},{16,20},{20,16},{24,28},{28,24},{1,5},{5... | collective-permute-start | bytes 393224 | tf_op jit(solution)/shard_map/ppermute | solution.py:278
  22.7 1.5 %collective-permute-start.6 = (bf16[8,8192]{1,0:T(8,128)(2,1)S(1)}, bf16[8,8192]{1,0:T(8,128)(2,1)S(1)}, u32[]{:S(2)}, u32[]{:S(2)}) collective-permute-start(bf16[8,8192]{1,0:T(8,128)(2,1)S(1)} %collective-permute-done.2.refs_11_), channel_id=1, source_target_pairs={{0,4},{4,0},{8,12},{12,8},{16,20},{20,16},{24,28},{28,24},{1,5},{5... | collective-permute-start | bytes 393224 | tf_op jit(solution)/shard_map/ppermute | solution.py:278
  38.7 8.4 %collective-permute-start.7 = (bf16[16,4096]{1,0:T(8,128)(2,1)S(1)}, bf16[16,4096]{1,0:T(8,128)(2,1)S(1)}, u32[]{:S(2)}, u32[]{:S(2)}) collective-permute-start(bf16[16,4096]{1,0:T(8,128)(2,1)S(1)} %get-tuple-element.30), channel_id=1, source_target_pairs={{0,3},{1,2},{2,1},{3,0},{4,7},{5,6},{6,5},{7,4},{8,11},{9,10},{10,... | collective-permute-start | bytes 393224 | tf_op jit(solution)/shard_map/ppermute | solution.py:278
  38.8 12.4 %collective-permute-start.8 = (bf16[16,4096]{1,0:T(8,128)(2,1)S(1)}, bf16[16,4096]{1,0:T(8,128)(2,1)S(1)}, u32[]{:S(2)}, u32[]{:S(2)}) collective-permute-start(bf16[16,4096]{1,0:T(8,128)(2,1)S(1)} %get-tuple-element.31), channel_id=1, source_target_pairs={{0,2},{1,3},{2,0},{3,1},{4,6},{5,7},{6,4},{7,5},{8,10},{9,11},{10,... | collective-permute-start | bytes 393224 | tf_op jit(solution)/shard_map/ppermute | solution.py:278
  38.9 12.3 %collective-permute-start.9 = (bf16[16,4096]{1,0:T(8,128)(2,1)S(1)}, bf16[16,4096]{1,0:T(8,128)(2,1)S(1)}, u32[]{:S(2)}, u32[]{:S(2)}) collective-permute-start(bf16[16,4096]{1,0:T(8,128)(2,1)S(1)} %get-tuple-element.32), channel_id=1, source_target_pairs={{0,1},{1,0},{2,3},{3,2},{4,5},{5,4},{6,7},{7,6},{8,9},{9,8},{10,11... | collective-permute-start | bytes 393224 | tf_op jit(solution)/shard_map/ppermute | solution.py:278
